TPU v7x, 256 devices: a whole 4x4x8 slice. The times are simulated.
256 devices in a mesh: band: 8 (over x, y_lo), grid: 32 (over y_hi, z, core).
Axes of the slice: x: 4, y: 4 (y_hi: 2, y_lo: 2; y = y_hi * 2 + y_lo), z: 8, core: 2. Of those that a mesh axis runs over, the one named last changes fastest.
Arguments:
- wavefunctions: bfloat16 [2048, 524288], P('band', 'grid'), may hold values from -6 to 6
- projectors: bfloat16 [2048, 8, 13, 256], P('grid'), may hold values from -0.0048828125 to 0.0048828125
- slot_atom: int32 [2048, 8], P('grid'), may hold values from -1 to 1023, as said below
- occupations: float32 [2048], P('band'), may hold values from 0.02 to 2
Outputs:
- density: float32 [1024, 13, 13], P('grid')
Inputs may be any that keep to these rules, and one draw needn't show every extreme that they name: `slot_atom`: -1 marks an empty slot. Any other entry is an atom a whose owning domain a // 32 lies within 3 domains, counted around the closed cycle of 32 domains, of the domain of the block, block index // 64. In every domain some block has all 8 slots filled.
All inputs are finite; a program needn't handle non-finite values.
Results may differ from a plain program's by a relative error of at most 0.0003.
Values sent between devices are 32-bit elements; how exact they have to be, the bound alone decides.
A program may use at most 64 MiB of HBM per device.

v0:
```python
import jax
import jax.numpy as jnp
from jax import lax
from jax.sharding import PartitionSpec as P

REACH = 3
ATOMS_DEV = 32


def shifted(block, axis, distance):
    devices = range(lax.axis_size(axis))
    route = [((i - distance) % len(devices), i) for i in devices]
    return lax.ppermute(block, axis, route)


def from_everyone(x, axis):
    devices = lax.axis_size(axis)
    return lax.all_to_all(jnp.broadcast_to(x[None], (devices, *x.shape)), axis, 0, 0, tiled=True)


def over_copies(x, axis):
    everything = from_everyone(x, axis)
    return jnp.sum(everything, axis=0)


def body(wavefunctions, projectors, slot_atom, occupations):
    band_count = wavefunctions.shape[0]
    block_count, capacity, proj_count, block_len = projectors.shape
    domains = lax.axis_size("grid")
    domain = lax.axis_index("grid")
    window_len = 2 * REACH + 1
    row_len = proj_count * band_count
    grid_blocks = wavefunctions.reshape(band_count, block_count, block_len)
    stacked = projectors.reshape(block_count, capacity * proj_count, block_len)
    slot_terms = jnp.einsum(
        "ngb,gcb->gcn", grid_blocks, stacked, preferred_element_type=jnp.float32
    )
    slot_terms = slot_terms.reshape(block_count * capacity, row_len)
    slot_ids = slot_atom.reshape(-1)
    owner = jnp.floor_divide(slot_ids, ATOMS_DEV)
    offset = jnp.mod(owner - domain + REACH, domains)
    target = jnp.where(
        slot_ids >= 0, offset * ATOMS_DEV + jnp.mod(slot_ids, ATOMS_DEV), window_len * ATOMS_DEV
    )
    selector = (
        jnp.arange(window_len * ATOMS_DEV, dtype=jnp.int32)[:, None] == target[None, :]
    ).astype(jnp.float32)
    window = jnp.dot(
        selector, slot_terms, precision=lax.Precision.HIGHEST, preferred_element_type=jnp.float32
    )
    window = window.reshape(window_len, ATOMS_DEV, row_len)
    forward = window[2 * REACH]
    for hop in range(REACH, 0, -1):
        forward = shifted(forward, "grid", 1) + window[REACH + hop - 1]
    backward = window[0]
    for hop in range(REACH, 0, -1):
        addend = window[REACH - hop + 1] if hop > 1 else jnp.zeros_like(backward)
        backward = shifted(backward, "grid", -1) + addend
    owned = forward + backward
    owned = owned.reshape(ATOMS_DEV, proj_count, band_count)
    weighted = owned * occupations.reshape(1, 1, band_count)
    partial_sum = jnp.einsum("ain,ajn->aij", weighted, owned, precision=lax.Precision.HIGHEST)
    density = over_copies(partial_sum, "band")
    return density


def solution(mesh):
    in_specs = (P("band", "grid"), P("grid", None, None, None), P("grid", None), P("band"))
    out_specs = P("grid", None, None)
    return jax.shard_map(body, mesh=mesh, in_specs=in_specs, out_specs=out_specs, check_vma=False)
```

profile of v0, /device:TPU:8, one launch (start us, length us, event | category | flops | bytes accessed | tf_op | source)
XLA Modules:
  0.0 78.7 jit_solution(8540286206186485369)
XLA Ops:
  0.0 2.8 %copy.11 = bf16[64,8,13,256]{3,0,2,1:T(8,128)(2,1)S(1)} copy(bf16[64,8,13,256]{3,1,2,0:T(8,128)(2,1)} %param.5) | data formatting | bytes 6815744 | tf_op args[1]
  2.8 9.4 %fusion = f32[64,104,256]{2,1,0:T(8,128)} fusion(bf16[32,64,8,256]{3,2,1,0:T(8,128)(2,1)} %bitcast.12, bf16[64,104,256]{2,0,1:T(8,128)(2,1)S(1)} %bitcast.11), kind=kOutput, calls=%fused_computation | convolution fusion | flops 872415232 | bytes 18612224 | tf_op jit(solution)/shard_map/ngb,gcb->gcn/dot_general | solution.py:35
  12.2 0.0 copy-start
  12.2 8.5 %reshape.104 = f32[512,3328]{1,0:T(8,128)} reshape(f32[64,104,256]{2,1,0:T(8,128)} %fusion) | data formatting | bytes 13631488 | tf_op jit(solution)/shard_map/reshape | solution.py:38
  20.6 0.0 copy-done
  20.6 0.1 copy.10
  20.7 0.1 reshape.101
  20.8 6.3 %fusion.6 = f32[224,3328]{1,0:T(8,128)S(1)} fusion(f32[512,3328]{1,0:T(8,128)} %reshape.104, s32[512]{0:T(512)S(1)} %fusion.15), kind=kOutput, calls=%fused_computation.7 | convolution fusion | flops 4580294656 | bytes 9799680 | tf_op jit(solution)/shard_map/dot_general | solution.py:48
  27.1 0.1 fusion.17
  27.2 0.1 collective-permute-start
  27.3 0.0 copy-start.1
  27.3 7.1 %collective-permute-start.3 = (f32[32,3328]{1,0:T(8,128)S(1)}, f32[32,3328]{1,0:T(8,128)S(1)}, u32[]{:S(2)}, u32[]{:S(2)}) collective-permute-start(f32[32,3328]{1,0:T(8,128)S(1)} %get-tuple-element.10), channel_id=1, source_target_pairs={{1,0},{2,1},{3,2},{4,3},{5,4},{6,5},{7,6},{8,7},{9,8},{10,9},{11,1... | collective-permute-start | bytes 1277960 | tf_op jit(solution)/shard_map/ppermute | solution.py:13
  34.4 5.7 %collective-permute-done = f32[32,3328]{1,0:T(8,128)S(1)} collective-permute-done((f32[32,3328]{1,0:T(8,128)S(1)}, f32[32,3328]{1,0:T(8,128)S(1)}, u32[]{:S(2)}, u32[]{:S(2)}) %collective-permute-start) | collective-permute-done | bytes 426016 | tf_op jit(solution)/shard_map/ppermute | solution.py:13
  40.1 0.0 collective-permute-done.3
  40.1 0.1 slice_add_fusion.4
  40.2 0.1 collective-permute-start.1
  40.3 5.5 %collective-permute-start.4 = (f32[32,3328]{1,0:T(8,128)S(1)}, f32[32,3328]{1,0:T(8,128)S(1)}, u32[]{:S(2)}, u32[]{:S(2)}) collective-permute-start(f32[32,3328]{1,0:T(8,128)S(1)} %get-tuple-element.8), channel_id=1, source_target_pairs={{1,0},{2,1},{3,2},{4,3},{5,4},{6,5},{7,6},{8,7},{9,8},{10,9},{11,1... | collective-permute-start | bytes 1277960 | tf_op jit(solution)/shard_map/ppermute | solution.py:13
  45.8 5.7 %collective-permute-done.1 = f32[32,3328]{1,0:T(8,128)S(1)} collective-permute-done((f32[32,3328]{1,0:T(8,128)S(1)}, f32[32,3328]{1,0:T(8,128)S(1)}, u32[]{:S(2)}, u32[]{:S(2)}) %collective-permute-start.1) | collective-permute-done | bytes 426016 | tf_op jit(solution)/shard_map/ppermute | solution.py:13
  51.6 0.0 collective-permute-done.4
  51.6 0.1 slice_add_fusion.3
  51.7 0.1 collective-permute-start.2
  51.8 5.7 %collective-permute-start.5 = (f32[32,3328]{1,0:T(8,128)S(1)}, f32[32,3328]{1,0:T(8,128)S(1)}, u32[]{:S(2)}, u32[]{:S(2)}) collective-permute-start(f32[32,3328]{1,0:T(8,128)S(1)} %get-tuple-element.6), channel_id=1, source_target_pairs={{1,0},{2,1},{3,2},{4,3},{5,4},{6,5},{7,6},{8,7},{9,8},{10,9},{11,1... | collective-permute-start | bytes 1277960 | tf_op jit(solution)/shard_map/ppermute | solution.py:13
  57.4 5.6 %collective-permute-done.2 = f32[32,3328]{1,0:T(8,128)S(1)} collective-permute-done((f32[32,3328]{1,0:T(8,128)S(1)}, f32[32,3328]{1,0:T(8,128)S(1)}, u32[]{:S(2)}, u32[]{:S(2)}) %collective-permute-start.2) | collective-permute-done | bytes 426016 | tf_op jit(solution)/shard_map/ppermute | solution.py:13
  63.0 0.1 collective-permute-done.5
  63.1 0.1 fusion.7
  63.2 0.1 reshape.105
  63.3 0.0 copy-done.1
  63.3 0.6 fusion.4
  63.9 0.2 copy.14
  64.1 0.1 broadcast_bitcast_fusion
  64.2 0.4 reshape.106
  64.6 11.5 %all_to_all.5 = f32[8,1,5408]{2,1,0:T(1,128)S(1)} all-to-all(f32[8,1,5408]{2,1,0:T(1,128)S(1)} %reshape.106), channel_id=1, replica_groups=mesh['band'=8,'grid'=32] {'band'}, dimensions={0} | all-to-all | bytes 346112 | tf_op jit(solution)/shard_map/all_to_all | solution.py:18
  76.1 0.5 broadcast.97
  76.6 1.1 %reduce = f32[8,5408]{1,0:T(8,128)S(1)} reduce(f32[8,1,5408]{2,1,0:T(1,128)S(1)} %all_to_all.5, f32[]{:T(128)} %broadcast.97), dimensions={1}, to_apply=%all_to_all.3.reduce_sub_computation | reduce | bytes 346116 | tf_op jit(solution)/shard_map/all_to_all | solution.py:18
  77.6 0.3 reshape.107
  78.0 0.7 bitcast_reduce_fusion
  (1 shorter events, 0.0 us)
Async XLA Ops:
  12.2 8.5 %copy-start = (s32[64,8]{0,1:T(8,128)S(1)}, s32[64,8]{0,1:T(8,128)}, u32[]{:S(2)}) copy-start(s32[64,8]{0,1:T(8,128)} %param.6) | copy-start | bytes 6148
  27.2 12.9 %collective-permute-start = (f32[32,3328]{1,0:T(8,128)S(1)}, f32[32,3328]{1,0:T(8,128)S(1)}, u32[]{:S(2)}, u32[]{:S(2)}) collective-permute-start(f32[32,3328]{1,0:T(8,128)S(1)} %get-tuple-element.9), channel_id=1, source_target_pairs={{31,0},{0,1},{1,2},{2,3},{3,4},{4,5},{5,6},{6,7},{7,8},{8,9},{9,10... | collective-permute-start | bytes 1277960 | tf_op jit(solution)/shard_map/ppermute | solution.py:13
  27.3 36.0 %copy-start.1 = (f32[256]{0:T(256)S(1)}, f32[256]{0:T(256)}, u32[]{:S(2)}) copy-start(f32[256]{0:T(256)} %param.7) | copy-start | bytes 3076
  27.3 12.8 %collective-permute-start.3 = (f32[32,3328]{1,0:T(8,128)S(1)}, f32[32,3328]{1,0:T(8,128)S(1)}, u32[]{:S(2)}, u32[]{:S(2)}) collective-permute-start(f32[32,3328]{1,0:T(8,128)S(1)} %get-tuple-element.10), channel_id=1, source_target_pairs={{1,0},{2,1},{3,2},{4,3},{5,4},{6,5},{7,6},{8,7},{9,8},{10,9},{11,1... | collective-permute-start | bytes 1277960 | tf_op jit(solution)/shard_map/ppermute | solution.py:13
  40.2 11.3 %collective-permute-start.1 = (f32[32,3328]{1,0:T(8,128)S(1)}, f32[32,3328]{1,0:T(8,128)S(1)}, u32[]{:S(2)}, u32[]{:S(2)}) collective-permute-start(f32[32,3328]{1,0:T(8,128)S(1)} %get-tuple-element.7), channel_id=1, source_target_pairs={{31,0},{0,1},{1,2},{2,3},{3,4},{4,5},{5,6},{6,7},{7,8},{8,9},{9,10... | collective-permute-start | bytes 1277960 | tf_op jit(solution)/shard_map/ppermute | solution.py:13
  40.3 11.3 %collective-permute-start.4 = (f32[32,3328]{1,0:T(8,128)S(1)}, f32[32,3328]{1,0:T(8,128)S(1)}, u32[]{:S(2)}, u32[]{:S(2)}) collective-permute-start(f32[32,3328]{1,0:T(8,128)S(1)} %get-tuple-element.8), channel_id=1, source_target_pairs={{1,0},{2,1},{3,2},{4,3},{5,4},{6,5},{7,6},{8,7},{9,8},{10,9},{11,1... | collective-permute-start | bytes 1277960 | tf_op jit(solution)/shard_map/ppermute | solution.py:13
  51.7 11.3 %collective-permute-start.2 = (f32[32,3328]{1,0:T(8,128)S(1)}, f32[32,3328]{1,0:T(8,128)S(1)}, u32[]{:S(2)}, u32[]{:S(2)}) collective-permute-start(f32[32,3328]{1,0:T(8,128)S(1)} %get-tuple-element.5), channel_id=1, source_target_pairs={{31,0},{0,1},{1,2},{2,3},{3,4},{4,5},{5,6},{6,7},{7,8},{8,9},{9,10... | collective-permute-start | bytes 1277960 | tf_op jit(solution)/shard_map/ppermute | solution.py:13
  51.8 11.3 %collective-permute-start.5 = (f32[32,3328]{1,0:T(8,128)S(1)}, f32[32,3328]{1,0:T(8,128)S(1)}, u32[]{:S(2)}, u32[]{:S(2)}) collective-permute-start(f32[32,3328]{1,0:T(8,128)S(1)} %get-tuple-element.6), channel_id=1, source_target_pairs={{1,0},{2,1},{3,2},{4,3},{5,4},{6,5},{7,6},{8,7},{9,8},{10,9},{11,1... | collective-permute-start | bytes 1277960 | tf_op jit(solution)/shard_map/ppermute | solution.py:13
where the time goes:
time: 79.1 us; the launch traced here: 78.7 us
  starting transfers between devices  18.6 us (24%)
  waiting for transfers between devices  17.1 us (22%)
  matrix products  16.3 us (21%)
  local copies, waits for them, and re-layouts  13.1 us (17%)
  blocking collectives  11.5 us (15%)
  other arithmetic  2.02 us (3%)
    ppermute x6, starting transfers between devices, shifted(): return lax.ppermute(block, axis, route)  18.6 us
    ppermute x6, waiting for transfers between devices, shifted(): return lax.ppermute(block, axis, route)  17.1 us
    all_to_all x1, blocking collectives, from_everyone(): lax.all_to_all(jnp.broadcast_to(x[None], (devices, *x.shape)), axis, 0, 0...  11.5 us
    dot_general x1, matrix products, body(): jnp.einsum('ngb,gcb->gcn', grid_blocks, stacked, preferred_element_type=j...  9.37 us
    reshape x1, local copies, waits for them, and re-layouts, body(): slot_terms = slot_terms.reshape(block_count * capacity, row_len)  8.49 us
    dot_general x1, matrix products, body(): jnp.dot(selector, slot_terms, precision=lax.Precision.HIGHEST, preferred_...  6.29 us
    unnamed x9, local copies, waits for them, and re-layouts  3.65 us
  transfers between devices with their start and end apart: 6, of which 4 were waited for; matrix products, arithmetic and copies ran while one was open for 0% of the time, Pallas kernels for 0%

commit v1 on v0

v1 whole, which is shorter than its diff:
```python
import functools

import jax
import jax.numpy as jnp
from jax import lax
from jax.experimental import pallas as pl
from jax.experimental.pallas import tpu as pltpu
from jax.sharding import PartitionSpec as P

REACH = 3
ATOMS_DEV = 32
NPROJ = 13
CAP = 8
NBLK = 64
BLK = 256
HALF = 128
WINDOW = 2 * REACH + 1
SLOTS = NBLK * CAP
GROUPS = ATOMS_DEV // 8
PIECES = 4
NT = (((1,), (1,)), ((), ()))
MESH = pl.DeviceIdType.MESH


def kernel(n_band, n_grid, target, occ, proj_hbm, wave_hbm, out, proj, wave, pick, high, low, window,
           landed, mine, gathered, proj_sem, wave_sem, send_sem, recv_sem, dsend_sem, drecv_sem):
    band = lax.axis_index("band")
    grid = lax.axis_index("grid")
    after = lax.rem(grid + 1, n_grid)
    before = lax.rem(grid + n_grid - 1, n_grid)

    barrier = pltpu.get_barrier_semaphore()
    for other in (after, before):
        pl.semaphore_signal(barrier, inc=1, device_id={"grid": other}, device_id_type=MESH)
    for step in range(1, n_band):
        pl.semaphore_signal(
            barrier, inc=1, device_id={"band": lax.rem(band + step, n_band)}, device_id_type=MESH
        )

    blocks = NBLK // PIECES
    cols = blocks * BLK
    proj_in, wave_in = [], [[], []]
    for k in range(PIECES):
        at = pl.ds(k * blocks, blocks)
        proj_in.append(pltpu.make_async_copy(proj_hbm.at[at], proj.at[at], proj_sem.at[k]))
    for h in range(2):
        for k in range(PIECES):
            at = (pl.ds(h * HALF, HALF), pl.ds(k * cols, cols))
            wave_in[h].append(pltpu.make_async_copy(wave_hbm.at[at], wave.at[at], wave_sem.at[h, k]))
    for k in range(PIECES):
        proj_in[k].start()
        wave_in[0][k].start()
    for k in range(PIECES):
        wave_in[1][k].start()

    rows = lax.broadcasted_iota(jnp.int32, (WINDOW * ATOMS_DEV, SLOTS), 0)
    pick[...] = jnp.where(rows == target[...], 1.0, 0.0).astype(jnp.bfloat16)

    def project(h):
        def two_blocks(pair):
            parts = []
            for g in (2 * pair, 2 * pair + 1):
                piece = wave[pl.ds(h * HALF, HALF), pl.ds(pl.multiple_of(g * BLK, BLK), BLK)]
                terms = lax.dot_general(proj[g], piece, NT, preferred_element_type=jnp.float32)
                parts.append(terms.reshape(NPROJ, CAP, HALF))
            terms = jnp.concatenate(parts, axis=1)
            top = terms.astype(jnp.bfloat16)
            rest = (terms - top.astype(jnp.float32)).astype(jnp.bfloat16)
            at = pl.ds(pl.multiple_of(pair * 16, 16), 16)
            for i in range(NPROJ):
                lanes = pl.ds(i % 2 * HALF, HALF)
                high[i // 2, at, lanes] = top[i]
                low[i // 2, at, lanes] = rest[i]

        for k in range(PIECES):
            if h == 0:
                proj_in[k].wait()
            wave_in[h][k].wait()

            def some(step, carry):
                for u in range(4):
                    two_blocks(k * (blocks // 2) + step * 4 + u)
                return carry

            lax.fori_loop(0, blocks // 8, some, 0)

    def select(h):
        for two in range((NPROJ + 1) // 2):
            width = 2 * HALF if two < NPROJ // 2 else HALF
            rows = jnp.dot(pick[...], high[two, :, :width], preferred_element_type=jnp.float32)
            rows += jnp.dot(pick[...], low[two, :, :width], preferred_element_type=jnp.float32)
            rows = rows.reshape(WINDOW * GROUPS, 8, width)
            for part in range(width // HALF):
                window[h, :, 2 * two + part] = rows[:, :, part * HALF:(part + 1) * HALF]

    def chunk(place, a):
        return pl.ds(place * GROUPS + 2 * a, 2)

    def send(phase, h, a, way):
        q = 2 * h + a
        place = 2 * phase + way
        return pltpu.make_async_remote_copy(
            src_ref=window.at[h, chunk(place, a)],
            dst_ref=landed.at[way, phase, q],
            send_sem=send_sem.at[way, phase, q],
            recv_sem=recv_sem.at[way, phase, q],
            device_id={"grid": after if way == 0 else before},
            device_id_type=MESH,
        )

    for h in range(2):
        project(h)
        select(h)
        if h == 0:
            pl.semaphore_wait(barrier, n_band + 1)
        for a in range(2):
            for way in range(2):
                send(0, h, a, way).start()

    for phase in (1, 2):
        for h in range(2):
            for a in range(2):
                for way in range(2):
                    send(phase - 1, h, a, way).wait_recv()
                    at = chunk(2 * phase + way, a)
                    window[h, at] = window[h, at] + landed[way, phase - 1, 2 * h + a]
                    send(phase, h, a, way).start()

    def share(step, a):
        other = lax.rem(band + step, n_band)
        return pltpu.make_async_remote_copy(
            src_ref=mine.at[a],
            dst_ref=gathered.at[n_band - 1 - step, a],
            send_sem=dsend_sem.at[step - 1, a],
            recv_sem=drecv_sem.at[step - 1, a],
            device_id={"band": other},
            device_id_type=MESH,
        )

    atom_of_row = lax.broadcasted_iota(jnp.int32, (NPROJ, 8, NPROJ * 8), 1)
    atom_of_lane = lax.broadcasted_iota(jnp.int32, (NPROJ, 8, NPROJ * 8), 2) % 8
    for h in range(2):
        weight = occ[:, h * HALF:(h + 1) * HALF]
        for a in range(2):
            q = 2 * h + a
            for way in range(2):
                send(2, h, a, way).wait_recv()
            for part in range(2):
                owned = window[h, 6 * GROUPS + 2 * a + part] + (landed[0, 2, q, part] + landed[1, 2, q, part])
                owned = owned.reshape(NPROJ * 8, HALF)
                gram = lax.dot_general(
                    owned, owned * weight, NT, precision=lax.Precision.HIGHEST,
                    preferred_element_type=jnp.float32,
                ).reshape(NPROJ, 8, NPROJ * 8)
                dens = jnp.sum(jnp.where(atom_of_row == atom_of_lane, gram, 0.0), axis=1)
                at = (a, part, slice(0, NPROJ), slice(0, NPROJ * 8))
                if h == 0:
                    mine[at] = dens
                else:
                    mine[at] = mine[at] + dens
            if h == 1:
                for step in range(1, n_band):
                    share(step, a).start()

    for a in range(2):
        for step in range(1, n_band):
            share(step, a).wait_recv()
        total = mine[a]
        for step in range(1, n_band):
            total = total + gathered[n_band - 1 - step, a]
        for i in range(NPROJ):
            for part in range(2):
                group = 2 * a + part
                out[i, :, group * 8:(group + 1) * 8] = total[part, :NPROJ, i * 8:(i + 1) * 8]

    for phase in range(3):
        for h in range(2):
            for a in range(2):
                for way in range(2):
                    send(phase, h, a, way).wait_send()
    for a in range(2):
        for step in range(1, n_band):
            share(step, a).wait_send()


def body(wavefunctions, projectors, slot_atom, occupations):
    n_band = lax.axis_size("band")
    n_grid = lax.axis_size("grid")
    domain = lax.axis_index("grid")
    stacked = jnp.transpose(projectors, (0, 2, 1, 3)).reshape(NBLK, NPROJ * CAP, BLK)
    offset = jnp.mod(jnp.floor_divide(slot_atom, ATOMS_DEV) - domain + REACH, n_grid)
    place = jnp.where(offset > REACH, 2 * (2 * REACH - offset), 2 * offset + 1)
    place = jnp.where(offset == REACH, 2 * REACH, place)
    target = jnp.where(slot_atom >= 0, place * ATOMS_DEV + jnp.mod(slot_atom, ATOMS_DEV), -1)
    vmem = pl.BlockSpec(memory_space=pltpu.VMEM)
    hbm = pl.BlockSpec(memory_space=pl.ANY)
    chunk = (2, NPROJ, 8, HALF)
    density = pl.pallas_call(
        functools.partial(kernel, n_band, n_grid),
        out_shape=jax.ShapeDtypeStruct((NPROJ, NPROJ, ATOMS_DEV), jnp.float32),
        in_specs=[vmem, vmem, hbm, hbm],
        out_specs=vmem,
        scratch_shapes=[
            pltpu.VMEM((NBLK, NPROJ * CAP, BLK), jnp.bfloat16),
            pltpu.VMEM((2 * HALF, NBLK * BLK), jnp.bfloat16),
            pltpu.VMEM((WINDOW * ATOMS_DEV, SLOTS), jnp.bfloat16),
            pltpu.VMEM(((NPROJ + 1) // 2, SLOTS, 2 * HALF), jnp.bfloat16),
            pltpu.VMEM(((NPROJ + 1) // 2, SLOTS, 2 * HALF), jnp.bfloat16),
            pltpu.VMEM((2, WINDOW * GROUPS, NPROJ, 8, HALF), jnp.float32),
            pltpu.VMEM((2, 3, 4) + chunk, jnp.float32),
            pltpu.VMEM((2, 2, 16, 128), jnp.float32),
            pltpu.VMEM((n_band - 1, 2, 2, 16, 128), jnp.float32),
            pltpu.SemaphoreType.DMA((PIECES,)),
            pltpu.SemaphoreType.DMA((2, PIECES)),
            pltpu.SemaphoreType.DMA((2, 3, 4)),
            pltpu.SemaphoreType.DMA((2, 3, 4)),
            pltpu.SemaphoreType.DMA((n_band - 1, 2)),
            pltpu.SemaphoreType.DMA((n_band - 1, 2)),
        ],
        compiler_params=pltpu.CompilerParams(collective_id=0, has_side_effects=True),
        name="density",
    )(target.reshape(1, SLOTS), occupations.reshape(1, 2 * HALF), stacked, wavefunctions)
    return jnp.transpose(density, (2, 0, 1))


def solution(mesh):
    in_specs = (P("band", "grid"), P("grid", None, None, None), P("grid", None), P("band"))
    out_specs = P("grid", None, None)
    return jax.shard_map(body, mesh=mesh, in_specs=in_specs, out_specs=out_specs, check_vma=False)
```

time: 79.1 us -> 41.9 us (0.53)
  Pallas kernels: 0 us -> 38.8 us
  starting transfers between devices: 18.6 us -> 0 us
  waiting for transfers between devices: 17.1 us -> 0 us
  matrix products: 16.3 us -> 0 us
  blocking collectives: 11.5 us -> 0 us
  local copies, waits for them, and re-layouts: 13.1 us -> 2.3 us
  other arithmetic: 2.02 us -> 0.71 us
    pallas_call x0 -> x1, Pallas kernels: none -> 38.8 us  [body(): pl.pallas_call(functools.partial(kernel, n_band, n_grid), out_shape=jax.S...]
    ppermute x6 -> x0, starting transfers between devices: 18.6 us -> none  [shifted(): return lax.ppermute(block, axis, route)]
    ppermute x6 -> x0, waiting for transfers between devices: 17.1 us -> none  [shifted(): return lax.ppermute(block, axis, route)]
    dot_general x3 -> x0, matrix products: 16.3 us -> none  [the longest x1 9.37 us: body(): jnp.einsum('ngb,gcb->gcn', grid_blocks, stacked, preferred_element_type=j...]
    all_to_all x1 -> x0, blocking collectives: 11.5 us -> none  [from_everyone(): lax.all_to_all(jnp.broadcast_to(x[None], (devices, *x.shape)), axis, 0, 0...]
    reshape x3 -> x1, local copies, waits for them, and re-layouts: 8.72 us -> 0.67 us  [body(): target.reshape(1, SLOTS)]
    unnamed x9 -> x1, local copies, waits for them, and re-layouts: 3.65 us -> 1.55 us
    all_to_all x1 -> x0, other arithmetic: 1.05 us -> none  [from_everyone(): lax.all_to_all(jnp.broadcast_to(x[None], (devices, *x.shape)), axis, 0, 0...]
  transfers between devices with their start and end apart: 6 -> 0, of which waited for: 4 -> 0; matrix products, arithmetic and copies ran while one was open for 0% -> 0% of each run, Pallas kernels for 0% -> 0%
where the time goes in v1:
time: 41.9 us; the launch traced here: 41.8 us
  Pallas kernels  38.8 us (93%)
  local copies, waits for them, and re-layouts  2.3 us (5%)
  other arithmetic  0.71 us (2%)
    pallas_call x1, Pallas kernels, body(): pl.pallas_call(functools.partial(kernel, n_band, n_grid), out_shape=jax.S...  38.8 us
    unnamed x1, local copies, waits for them, and re-layouts  1.55 us

profile of v1, /device:TPU:8, one launch (start us, length us, event | category | flops | bytes accessed | tf_op | source)
XLA Modules:
  0.0 41.8 jit_solution(3680057328841842714)
XLA Ops:
  0.0 0.7 %fusion.4 = s32[64,8]{0,1:T(8,128)S(1)} fusion(s32[64,8]{0,1:T(8,128)} %param.6, s32[]{:T(128)S(6)} %axis_index.12), kind=kLoop, calls=%fused_computation.12 | loop fusion | flops 22528 | bytes 4100 | tf_op jit(solution)/shard_map/jit(_where)/select_n | solution.py:194
  0.7 0.1 copy.6
  0.8 0.7 %reshape.9.target = s32[1,512]{1,0:T(1,128)} reshape(s32[64,8]{1,0:T(8,128)S(1)} %copy.6) | data formatting | bytes 4096 | tf_op jit(solution)/shard_map/reshape | solution.py:222
  1.5 38.8 %density.1 = f32[13,13,32]{2,1,0:T(8,128)} custom-call(s32[1,512]{1,0:T(1,128)} %reshape.9.target, f32[1,256]{1,0:T(1,128)} %bitcast.7, bf16[64,104,256]{2,1,0:T(8,128)(2,1)} %bitcast.5, bf16[256,16384]{1,0:T(8,128)(2,1)} %wave_hbm.1), custom_call_target="tpu_custom_call" | custom-call | tf_op jit(solution)/shard_map/density/pallas_call | solution.py:198
  40.2 1.5 %copy.8 = f32[32,13,13]{0,2,1:T(8,128)} copy(f32[32,13,13]{0,2,1:T(8,128)} %bitcast.6) | data formatting | bytes 43264

commit v2 on v1

--- a/solution.py
+++ b/solution.py
@@ -17,13 +17,15 @@
 WINDOW = 2 * REACH + 1
 SLOTS = NBLK * CAP
 GROUPS = ATOMS_DEV // 8
+VMEM_LIMIT = 55000000
+AHEAD = 2
 PIECES = 4
 NT = (((1,), (1,)), ((), ()))
 MESH = pl.DeviceIdType.MESH
 
 
-def kernel(n_band, n_grid, target, occ, proj_hbm, wave_hbm, out, proj, wave, pick, high, low, window,
-           landed, mine, gathered, proj_sem, wave_sem, send_sem, recv_sem, dsend_sem, drecv_sem):
+def kernel(n_band, n_grid, slot_hbm, occ_hbm, proj_hbm, wave_hbm, out, slot, occ, proj, wave, pick, high, low, window,
+           landed, mine, gathered, small_sem, proj_sem, wave_sem, send_sem, recv_sem, dsend_sem, drecv_sem):
     band = lax.axis_index("band")
     grid = lax.axis_index("grid")
     after = lax.rem(grid + 1, n_grid)
@@ -47,51 +49,74 @@
         for k in range(PIECES):
             at = (pl.ds(h * HALF, HALF), pl.ds(k * cols, cols))
             wave_in[h].append(pltpu.make_async_copy(wave_hbm.at[at], wave.at[at], wave_sem.at[h, k]))
-    for k in range(PIECES):
-        proj_in[k].start()
-        wave_in[0][k].start()
-    for k in range(PIECES):
-        wave_in[1][k].start()
-
+    slot_in = pltpu.make_async_copy(slot_hbm, slot, small_sem.at[0])
+    occ_in = pltpu.make_async_copy(occ_hbm, occ, small_sem.at[1])
+    slot_in.start()
+    loads = [[proj_in[k], wave_in[0][k]] for k in range(PIECES)] + [[wave_in[1][k]] for k in range(PIECES)]
+    loads[-1].append(occ_in)
+    for copies in loads[:AHEAD]:
+        for copy in copies:
+            copy.start()
+
+    slot_in.wait()
+    ids = slot[...]
+    offset = (ids >> 5) - grid
+    offset = jnp.where(offset > n_grid // 2, offset - n_grid, offset)
+    offset = jnp.where(offset < -(n_grid // 2), offset + n_grid, offset)
+    place = jnp.where(offset > 0, 2 * (REACH - offset), 2 * (REACH + offset) + 1)
+    place = jnp.where(offset == 0, 2 * REACH, place)
+    target = jnp.where(ids >= 0, place * ATOMS_DEV + (ids & (ATOMS_DEV - 1)), -1)
+    spread = lax.broadcasted_iota(jnp.int32, (NBLK, SLOTS), 1) >> 3
+    spread = (spread == lax.broadcasted_iota(jnp.int32, (NBLK, SLOTS), 0)).astype(jnp.float32)
+    target = jnp.dot(
+        target.astype(jnp.float32).astype(jnp.bfloat16), spread.astype(jnp.bfloat16),
+        preferred_element_type=jnp.float32,
+    )
+    own_slot = (lax.broadcasted_iota(jnp.int32, (CAP, SLOTS), 1) & 7) == lax.broadcasted_iota(
+        jnp.int32, (CAP, SLOTS), 0
+    )
+    target = jnp.sum(jnp.where(own_slot, target, 0.0), axis=0, keepdims=True).astype(jnp.int32)
     rows = lax.broadcasted_iota(jnp.int32, (WINDOW * ATOMS_DEV, SLOTS), 0)
-    pick[...] = jnp.where(rows == target[...], 1.0, 0.0).astype(jnp.bfloat16)
+    pick[...] = jnp.where(rows == target, 1.0, 0.0).astype(jnp.bfloat16)
 
     def project(h):
         def two_blocks(pair):
             parts = []
             for g in (2 * pair, 2 * pair + 1):
-                piece = wave[pl.ds(h * HALF, HALF), pl.ds(pl.multiple_of(g * BLK, BLK), BLK)]
+                piece = wave[pl.ds(h * HALF, HALF), pl.ds(g * BLK, BLK)]
                 terms = lax.dot_general(proj[g], piece, NT, preferred_element_type=jnp.float32)
                 parts.append(terms.reshape(NPROJ, CAP, HALF))
             terms = jnp.concatenate(parts, axis=1)
             top = terms.astype(jnp.bfloat16)
             rest = (terms - top.astype(jnp.float32)).astype(jnp.bfloat16)
-            at = pl.ds(pl.multiple_of(pair * 16, 16), 16)
+            at = pl.ds(pair * 16, 16)
             for i in range(NPROJ):
                 lanes = pl.ds(i % 2 * HALF, HALF)
                 high[i // 2, at, lanes] = top[i]
                 low[i // 2, at, lanes] = rest[i]
 
         for k in range(PIECES):
-            if h == 0:
-                proj_in[k].wait()
-            wave_in[h][k].wait()
-
-            def some(step, carry):
-                for u in range(4):
-                    two_blocks(k * (blocks // 2) + step * 4 + u)
-                return carry
-
-            lax.fori_loop(0, blocks // 8, some, 0)
-
-    def select(h):
+            turn = h * PIECES + k
+            for copy in loads[turn]:
+                copy.wait()
+            for copy in loads[turn + AHEAD] if turn + AHEAD < len(loads) else ():
+                copy.start()
+            for pair in range(blocks // 2):
+                two_blocks(k * (blocks // 2) + pair)
+            if k % 2 == 1:
+                select(h, k // 2)
+
+    def select(h, part):
+        at = slice(part * SLOTS // 2, (part + 1) * SLOTS // 2)
         for two in range((NPROJ + 1) // 2):
             width = 2 * HALF if two < NPROJ // 2 else HALF
-            rows = jnp.dot(pick[...], high[two, :, :width], preferred_element_type=jnp.float32)
-            rows += jnp.dot(pick[...], low[two, :, :width], preferred_element_type=jnp.float32)
+            rows = jnp.dot(pick[:, at], high[two, at, :width], preferred_element_type=jnp.float32)
+            rows += jnp.dot(pick[:, at], low[two, at, :width], preferred_element_type=jnp.float32)
             rows = rows.reshape(WINDOW * GROUPS, 8, width)
-            for part in range(width // HALF):
-                window[h, :, 2 * two + part] = rows[:, :, part * HALF:(part + 1) * HALF]
+            for lane in range(width // HALF):
+                i = 2 * two + lane
+                sums = rows[:, :, lane * HALF:(lane + 1) * HALF]
+                window[h, :, i] = sums if part == 0 else window[h, :, i] + sums
 
     def chunk(place, a):
         return pl.ds(place * GROUPS + 2 * a, 2)
@@ -110,7 +135,6 @@
 
     for h in range(2):
         project(h)
-        select(h)
         if h == 0:
             pl.semaphore_wait(barrier, n_band + 1)
         for a in range(2):
@@ -186,21 +210,18 @@
 def body(wavefunctions, projectors, slot_atom, occupations):
     n_band = lax.axis_size("band")
     n_grid = lax.axis_size("grid")
-    domain = lax.axis_index("grid")
     stacked = jnp.transpose(projectors, (0, 2, 1, 3)).reshape(NBLK, NPROJ * CAP, BLK)
-    offset = jnp.mod(jnp.floor_divide(slot_atom, ATOMS_DEV) - domain + REACH, n_grid)
-    place = jnp.where(offset > REACH, 2 * (2 * REACH - offset), 2 * offset + 1)
-    place = jnp.where(offset == REACH, 2 * REACH, place)
-    target = jnp.where(slot_atom >= 0, place * ATOMS_DEV + jnp.mod(slot_atom, ATOMS_DEV), -1)
     vmem = pl.BlockSpec(memory_space=pltpu.VMEM)
-    hbm = pl.BlockSpec(memory_space=pl.ANY)
+    hbm = pl.BlockSpec(memory_space=pltpu.HBM)
     chunk = (2, NPROJ, 8, HALF)
     density = pl.pallas_call(
         functools.partial(kernel, n_band, n_grid),
         out_shape=jax.ShapeDtypeStruct((NPROJ, NPROJ, ATOMS_DEV), jnp.float32),
-        in_specs=[vmem, vmem, hbm, hbm],
+        in_specs=[hbm] * 4,
         out_specs=vmem,
         scratch_shapes=[
+            pltpu.VMEM((CAP, NBLK), jnp.int32),
+            pltpu.VMEM((1, 2 * HALF), jnp.float32),
             pltpu.VMEM((NBLK, NPROJ * CAP, BLK), jnp.bfloat16),
             pltpu.VMEM((2 * HALF, NBLK * BLK), jnp.bfloat16),
             pltpu.VMEM((WINDOW * ATOMS_DEV, SLOTS), jnp.bfloat16),
@@ -210,6 +231,7 @@
             pltpu.VMEM((2, 3, 4) + chunk, jnp.float32),
             pltpu.VMEM((2, 2, 16, 128), jnp.float32),
             pltpu.VMEM((n_band - 1, 2, 2, 16, 128), jnp.float32),
+            pltpu.SemaphoreType.DMA((2,)),
             pltpu.SemaphoreType.DMA((PIECES,)),
             pltpu.SemaphoreType.DMA((2, PIECES)),
             pltpu.SemaphoreType.DMA((2, 3, 4)),
@@ -217,9 +239,9 @@
             pltpu.SemaphoreType.DMA((n_band - 1, 2)),
             pltpu.SemaphoreType.DMA((n_band - 1, 2)),
         ],
-        compiler_params=pltpu.CompilerParams(collective_id=0, has_side_effects=True),
+        compiler_params=pltpu.CompilerParams(collective_id=0, has_side_effects=True, vmem_limit_bytes=VMEM_LIMIT),
         name="density",
-    )(target.reshape(1, SLOTS), occupations.reshape(1, 2 * HALF), stacked, wavefunctions)
+    )(*(pltpu.with_memory_space_constraint(x, pltpu.HBM) for x in (slot_atom.T, occupations.reshape(1, 2 * HALF), stacked, wavefunctions)))
     return jnp.transpose(density, (2, 0, 1))
 
 

time: 41.9 us -> 36.5 us (0.87)
  Pallas kernels: 38.8 us -> 35.7 us
  local copies, waits for them, and re-layouts: 2.3 us -> 0.65 us
  other arithmetic: 0.71 us -> 0 us
    pallas_call x1, Pallas kernels: 38.8 us -> 35.7 us  [body(): pl.pallas_call(functools.partial(kernel, n_band, n_grid), out_shape=jax.S...]
    unnamed x1, local copies, waits for them, and re-layouts: 1.55 us -> 0.65 us
    select_n x1 -> x0, other arithmetic: 0.71 us -> none  [body(): jnp.where(slot_atom >= 0, place * ATOMS_DEV + jnp.mod(slot_atom, ATOMS_DE...]
    reshape x1 -> x0, local copies, waits for them, and re-layouts: 0.67 us -> none  [body(): target.reshape(1, SLOTS)]
where the time goes in v2:
time: 36.5 us; the launch traced here: 36.4 us
  Pallas kernels  35.7 us (98%)
  local copies, waits for them, and re-layouts  0.65 us (2%)
    pallas_call x1, Pallas kernels, body(): pl.pallas_call(functools.partial(kernel, n_band, n_grid), out_shape=jax.S...  35.7 us

profile of v2, /device:TPU:8, one launch (start us, length us, event | category | flops | bytes accessed | tf_op | source)
XLA Modules:
  0.0 36.4 jit_solution(9116559526813033132)
XLA Ops:
  0.0 35.7 %density.1 = f32[13,13,32]{2,1,0:T(8,128)S(1)} custom-call(s32[8,64]{1,0:T(8,128)} %bitcast.8, f32[1,256]{1,0:T(1,128)} %bitcast.9, bf16[64,104,256]{2,1,0:T(8,128)(2,1)} %bitcast.7, bf16[256,16384]{1,0:T(8,128)(2,1)} %wave_hbm.1), custom_call_target="tpu_custom_call" | custom-call | tf_op jit(solution)/shard_map/density/pallas_call | solution.py:217
  35.7 0.6 %copy.6 = f32[32,13,13]{0,2,1:T(8,128)} copy(f32[32,13,13]{0,2,1:T(8,128)S(1)} %bitcast.6) | data formatting | bytes 43264

commit v3 on v2

--- a/solution.py
+++ b/solution.py
@@ -18,14 +18,15 @@
 SLOTS = NBLK * CAP
 GROUPS = ATOMS_DEV // 8
 VMEM_LIMIT = 55000000
-AHEAD = 2
-PIECES = 4
+AHEAD = (3, 0, 1, 1, 0)
+PIECES = ((12, 20, 32), (64,))
 NT = (((1,), (1,)), ((), ()))
 MESH = pl.DeviceIdType.MESH
 
 
 def kernel(n_band, n_grid, slot_hbm, occ_hbm, proj_hbm, wave_hbm, out, slot, occ, proj, wave, pick, high, low, window,
-           landed, mine, gathered, small_sem, proj_sem, wave_sem, send_sem, recv_sem, dsend_sem, drecv_sem):
+           landed, mine, gathered, small_sem, proj_sem, wave_sem, send_sem, recv_sem, lsend_sem, lrecv_sem,
+           dsend_sem, drecv_sem):
     band = lax.axis_index("band")
     grid = lax.axis_index("grid")
     after = lax.rem(grid + 1, n_grid)
@@ -39,24 +40,30 @@
             barrier, inc=1, device_id={"band": lax.rem(band + step, n_band)}, device_id_type=MESH
         )
 
-    blocks = NBLK // PIECES
-    cols = blocks * BLK
-    proj_in, wave_in = [], [[], []]
-    for k in range(PIECES):
-        at = pl.ds(k * blocks, blocks)
-        proj_in.append(pltpu.make_async_copy(proj_hbm.at[at], proj.at[at], proj_sem.at[k]))
-    for h in range(2):
-        for k in range(PIECES):
-            at = (pl.ds(h * HALF, HALF), pl.ds(k * cols, cols))
-            wave_in[h].append(pltpu.make_async_copy(wave_hbm.at[at], wave.at[at], wave_sem.at[h, k]))
     slot_in = pltpu.make_async_copy(slot_hbm, slot, small_sem.at[0])
     occ_in = pltpu.make_async_copy(occ_hbm, occ, small_sem.at[1])
     slot_in.start()
-    loads = [[proj_in[k], wave_in[0][k]] for k in range(PIECES)] + [[wave_in[1][k]] for k in range(PIECES)]
-    loads[-1].append(occ_in)
-    for copies in loads[:AHEAD]:
-        for copy in copies:
-            copy.start()
+    loads = []
+    for h in range(2):
+        first = 0
+        for k, blocks in enumerate(PIECES[h]):
+            at = pl.ds(first, blocks)
+            cols = (pl.ds(h * HALF, HALF), pl.ds(first * BLK, blocks * BLK))
+            copies = [pltpu.make_async_copy(wave_hbm.at[cols], wave.at[cols], wave_sem.at[h, k])]
+            if h == 0:
+                copies.append(pltpu.make_async_copy(proj_hbm.at[at], proj.at[at], proj_sem.at[k]))
+            loads.append((first, blocks, copies))
+            first += blocks
+    loads[-1][2].append(occ_in)
+    waiting = list(loads)
+
+    def issue(count):
+        for _ in range(min(count, len(waiting))):
+            first, blocks, copies = waiting.pop(0)
+            for copy in copies:
+                copy.start(priority=int(len(waiting) < len(PIECES[1])))
+
+    issue(AHEAD[0])
 
     slot_in.wait()
     ids = slot[...]
@@ -95,16 +102,16 @@
                 high[i // 2, at, lanes] = top[i]
                 low[i // 2, at, lanes] = rest[i]
 
-        for k in range(PIECES):
-            turn = h * PIECES + k
-            for copy in loads[turn]:
+        for k in range(len(PIECES[h])):
+            turn = h * len(PIECES[0]) + k
+            first, blocks, copies = loads[turn]
+            for copy in copies:
                 copy.wait()
-            for copy in loads[turn + AHEAD] if turn + AHEAD < len(loads) else ():
-                copy.start()
-            for pair in range(blocks // 2):
-                two_blocks(k * (blocks // 2) + pair)
-            if k % 2 == 1:
-                select(h, k // 2)
+            issue(AHEAD[turn + 1])
+            for pair in range(first // 2, (first + blocks) // 2):
+                two_blocks(pair)
+                if pair % (NBLK // 4) == NBLK // 4 - 1:
+                    select(h, pair // (NBLK // 4))
 
     def select(h, part):
         at = slice(part * SLOTS // 2, (part + 1) * SLOTS // 2)
@@ -133,6 +140,17 @@
             device_id_type=MESH,
         )
 
+    def last(h, a, way, part):
+        q = 2 * h + a
+        return pltpu.make_async_remote_copy(
+            src_ref=window.at[h, (4 + way) * GROUPS + 2 * a + part],
+            dst_ref=landed.at[way, 2, q, part],
+            send_sem=lsend_sem.at[way, q, part],
+            recv_sem=lrecv_sem.at[way, q, part],
+            device_id={"grid": after if way == 0 else before},
+            device_id_type=MESH,
+        )
+
     for h in range(2):
         project(h)
         if h == 0:
@@ -148,7 +166,11 @@
                     send(phase - 1, h, a, way).wait_recv()
                     at = chunk(2 * phase + way, a)
                     window[h, at] = window[h, at] + landed[way, phase - 1, 2 * h + a]
-                    send(phase, h, a, way).start()
+                    if phase == 1:
+                        send(phase, h, a, way).start()
+                    else:
+                        for part in range(2):
+                            last(h, a, way, part).start()
 
     def share(step, a):
         other = lax.rem(band + step, n_band)
@@ -161,15 +183,17 @@
             device_id_type=MESH,
         )
 
+    steps = sorted(range(1, n_band), key=lambda step: abs(step - n_band // 2))
+
     atom_of_row = lax.broadcasted_iota(jnp.int32, (NPROJ, 8, NPROJ * 8), 1)
     atom_of_lane = lax.broadcasted_iota(jnp.int32, (NPROJ, 8, NPROJ * 8), 2) % 8
     for h in range(2):
         weight = occ[:, h * HALF:(h + 1) * HALF]
         for a in range(2):
             q = 2 * h + a
-            for way in range(2):
-                send(2, h, a, way).wait_recv()
             for part in range(2):
+                for way in range(2):
+                    last(h, a, way, part).wait_recv()
                 owned = window[h, 6 * GROUPS + 2 * a + part] + (landed[0, 2, q, part] + landed[1, 2, q, part])
                 owned = owned.reshape(NPROJ * 8, HALF)
                 gram = lax.dot_general(
@@ -183,25 +207,27 @@
                 else:
                     mine[at] = mine[at] + dens
             if h == 1:
-                for step in range(1, n_band):
+                for step in steps:
                     share(step, a).start()
 
     for a in range(2):
         for step in range(1, n_band):
             share(step, a).wait_recv()
-        total = mine[a]
-        for step in range(1, n_band):
-            total = total + gathered[n_band - 1 - step, a]
-        for i in range(NPROJ):
-            for part in range(2):
-                group = 2 * a + part
-                out[i, :, group * 8:(group + 1) * 8] = total[part, :NPROJ, i * 8:(i + 1) * 8]
-
-    for phase in range(3):
-        for h in range(2):
-            for a in range(2):
-                for way in range(2):
+        for part in range(2):
+            total = mine[a, part]
+            for step in range(1, n_band):
+                total = total + gathered[n_band - 1 - step, a, part]
+            group = 2 * a + part
+            for i in range(NPROJ):
+                out[i, :, group * 8:(group + 1) * 8] = total[:NPROJ, i * 8:(i + 1) * 8]
+
+    for h in range(2):
+        for a in range(2):
+            for way in range(2):
+                for phase in range(2):
                     send(phase, h, a, way).wait_send()
+                for part in range(2):
+                    last(h, a, way, part).wait_send()
     for a in range(2):
         for step in range(1, n_band):
             share(step, a).wait_send()
@@ -232,10 +258,12 @@
             pltpu.VMEM((2, 2, 16, 128), jnp.float32),
             pltpu.VMEM((n_band - 1, 2, 2, 16, 128), jnp.float32),
             pltpu.SemaphoreType.DMA((2,)),
-            pltpu.SemaphoreType.DMA((PIECES,)),
-            pltpu.SemaphoreType.DMA((2, PIECES)),
-            pltpu.SemaphoreType.DMA((2, 3, 4)),
-            pltpu.SemaphoreType.DMA((2, 3, 4)),
+            pltpu.SemaphoreType.DMA((len(PIECES[0]),)),
+            pltpu.SemaphoreType.DMA((2, max(len(p) for p in PIECES))),
+            pltpu.SemaphoreType.DMA((2, 2, 4)),
+            pltpu.SemaphoreType.DMA((2, 2, 4)),
+            pltpu.SemaphoreType.DMA((2, 4, 2)),
+            pltpu.SemaphoreType.DMA((2, 4, 2)),
             pltpu.SemaphoreType.DMA((n_band - 1, 2)),
             pltpu.SemaphoreType.DMA((n_band - 1, 2)),
         ],

time: 36.5 us -> 36.2 us (level)
  no operation moved by 1% of the time
where the time goes in v3:
time: 36.2 us; the launch traced here: 36.1 us
  Pallas kernels  35.4 us (98%)
  local copies, waits for them, and re-layouts  0.65 us (2%)
    pallas_call x1, Pallas kernels, body(): pl.pallas_call(functools.partial(kernel, n_band, n_grid), out_shape=jax.S...  35.4 us

profile of v3, /device:TPU:8, one launch (start us, length us, event | category | flops | bytes accessed | tf_op | source)
XLA Modules:
  0.0 36.1 jit_solution(4168466919277185814)
XLA Ops:
  0.0 35.4 %density.1 = f32[13,13,32]{2,1,0:T(8,128)S(1)} custom-call(s32[8,64]{1,0:T(8,128)} %bitcast.8, f32[1,256]{1,0:T(1,128)} %bitcast.9, bf16[64,104,256]{2,1,0:T(8,128)(2,1)} %bitcast.7, bf16[256,16384]{1,0:T(8,128)(2,1)} %wave_hbm.1), custom_call_target="tpu_custom_call" | custom-call | tf_op jit(solution)/shard_map/density/pallas_call | solution.py:243
  35.4 0.6 %copy.6 = f32[32,13,13]{0,2,1:T(8,128)} copy(f32[32,13,13]{0,2,1:T(8,128)S(1)} %bitcast.6) | data formatting | bytes 43264
